TPU v7x, 32 devices: a whole 2x2x4 slice. The times are simulated.
32 devices in a mesh: row: 4 (over z), col: 8 (over y, x, core).
Axes of the slice: x: 2, y: 2, z: 4, core: 2. Of those that a mesh axis runs over, the one named last changes fastest.
Arguments:
- fine_residual: bfloat16 [16, 524288], P(None, ('row', 'col')), may hold values from -6 to 6
- tiles_one: bfloat16 [8192, 128, 128], P(('row', 'col')), may hold values from -0.1875 to 0.1875
- pointers_one: int32 [4128], P(('row', 'col')), may hold values from 0 to 256, as said below
- columns_one: int32 [8192], P(('row', 'col')), may hold values from 0 to 1023, as said below
- points_one: int32 [131072], P(('col', 'row')), may hold values from 0 to 16383, as said below
- tiles_two: bfloat16 [4096, 128, 128], P(('row', 'col')), may hold values from -0.125 to 0.125
- pointers_two: int32 [2080], P(('row', 'col')), may hold values from 0 to 128, as said below
- columns_two: int32 [4096], P(('row', 'col')), may hold values from 0 to 127
- points_two: int32 [32768], P(('row', 'col')), may hold values from 0 to 4095, as said below
- tiles_three: bfloat16 [512, 128, 128], P(('row', 'col')), may hold values from -0.1875 to 0.1875
- pointers_three: int32 [288], P(('row', 'col')), may hold values from 0 to 16, as said below
- columns_three: int32 [512], P(('row', 'col')), may hold values from 0 to 63
- points_three: int32 [8192], P(('col', 'row')), may hold values from 0 to 1023, as said below
Outputs:
- coarse_one: bfloat16 [16, 131072], P(None, ('col', 'row'))
- coarse_two: bfloat16 [16, 32768], P(None, ('row', 'col'))
- coarse_three: bfloat16 [16, 8192], P(None, ('col', 'row'))
Inputs may be any that keep to these rules, and one draw needn't show every extreme that they name: `pointers_one`: each tile set's 128 + 1 pointers start at 0 and never fall; the last is that set's live slot count, at most 256; some set has 256 live slots. `pointers_two`: each tile set's 64 + 1 pointers start at 0 and never fall; the last is that set's live slot count, at most 128; some set has 128 live slots. `pointers_three`: each tile set's 8 + 1 pointers start at 0 and never fall; the last is that set's live slot count, at most 16; some set has 16 live slots. `columns_one`: among the live slots of one tile set, at most 32 name block columns with the same quotient by 128; some set reaches 32. `points_one`: values are distinct within each aligned run of 4096 entries. `points_two`: values are distinct within each aligned run of 1024 entries. `points_three`: values are distinct within each aligned run of 256 entries.
All inputs are finite; a program needn't handle non-finite values.
Results may differ from a plain program's by a relative error of at most 0.0057.
Values may be sent and summed in bfloat16 or wider, within the bound.
No kernel may reach another device: no remote copies, remote signals or barrier semaphores. Data moves between devices by JAX's collectives and lax.ppermute only.
A program may use at most 128 MiB of HBM per device.

v0:
```python
import jax
import jax.numpy as jnp
from jax import lax
from jax.sharding import PartitionSpec as P


def slot_layout(pointers, slot_count):
    block_count = pointers.shape[0] - 1
    positions = jnp.arange(slot_count, dtype=jnp.int32)
    is_live = positions < pointers[block_count]
    finished = jnp.sum((pointers[1:][None, :] <= positions[:, None]).astype(jnp.int32), axis=1)
    segment = jnp.where(is_live, finished, block_count)
    return (is_live, segment)


def block_sums(products, segment, block_count):
    summed = jax.ops.segment_sum(
        products, segment, num_segments=block_count + 1, indices_are_sorted=True
    )
    summed = summed[:block_count]
    return jnp.transpose(summed, (1, 0, 2)).reshape(summed.shape[1], block_count * summed.shape[2])


def group_products(tiles, fine_group, columns, segment, block_count):
    vector_count = fine_group.shape[0]
    tile_edge = tiles.shape[1]
    blocks = fine_group.reshape(vector_count, fine_group.shape[1] // tile_edge, tile_edge)
    picked = jnp.take(blocks, columns, axis=1)
    products = jnp.einsum("sij,vsj->svi", tiles, picked, preferred_element_type=jnp.float32)
    return block_sums(products, segment, block_count)


def add_points(partial_value, own_piece, points, position):
    injected = jnp.take(own_piece, points, axis=1).astype(jnp.float32)
    offset = position * points.shape[0]
    current = lax.dynamic_slice_in_dim(partial_value, offset, points.shape[0], 1)
    return lax.dynamic_update_slice_in_dim(partial_value, current + injected, offset, 1)


def on_device(
    fine_residual,
    tiles_one,
    pointers_one,
    columns_one,
    points_one,
    tiles_two,
    pointers_two,
    columns_two,
    points_two,
    tiles_three,
    pointers_three,
    columns_three,
    points_three,
):
    tile_edge = tiles_one.shape[1]
    vector_count = fine_residual.shape[0]
    slots_first = tiles_one.shape[0]
    blocks_first = pointers_one.shape[0] - 1
    live_first, segment_first = slot_layout(pointers_one, slots_first)
    peer_count = lax.axis_size("col")
    per_peer = slots_first // peer_count
    blocks_peer = fine_residual.shape[1] // tile_edge
    owner_peer = columns_one // blocks_peer
    within = columns_one % blocks_peer
    peer_ids = jnp.arange(peer_count, dtype=jnp.int32)
    peer_hits = ((owner_peer[:, None] == peer_ids[None, :]) & live_first[:, None]).astype(jnp.int32)
    peer_rank = jnp.sum(jnp.cumsum(peer_hits, axis=0) * peer_hits, axis=1) - 1
    target = jnp.where(live_first, owner_peer * per_peer + peer_rank, peer_count * per_peer)
    requests = jnp.zeros((peer_count * per_peer,), jnp.int32).at[target].set(within, mode="drop")
    requests = requests.reshape(peer_count, per_peer)
    own_blocks = jnp.transpose(
        fine_residual.reshape(vector_count, blocks_peer, tile_edge), (1, 0, 2)
    )
    found_blocks = jnp.take(
        own_blocks, lax.all_to_all(requests, "col", split_axis=0, concat_axis=0, tiled=True), axis=0
    )
    replies = lax.all_to_all(found_blocks, "col", split_axis=0, concat_axis=0, tiled=True)
    flat_replies = replies.reshape(peer_count * per_peer, vector_count, tile_edge)
    picked = jnp.take(flat_replies, jnp.minimum(target, peer_count * per_peer - 1), axis=0)
    products = jnp.einsum("sij,svj->svi", tiles_one, picked, preferred_element_type=jnp.float32)
    partial_one = block_sums(products, segment_first, blocks_first)
    partial_one = add_points(partial_one, fine_residual, points_one, lax.axis_index("row"))
    coarse_one = lax.psum_scatter(partial_one, "row", scatter_dimension=1, tiled=True).astype(
        jnp.bfloat16
    )
    group_one = lax.all_gather(coarse_one, "row", axis=1, tiled=True)
    segment_second = slot_layout(pointers_two, tiles_two.shape[0])[1]
    partial_two = group_products(
        tiles_two, group_one, columns_two, segment_second, pointers_two.shape[0] - 1
    )
    partial_two = add_points(partial_two, coarse_one, points_two, lax.axis_index("col"))
    coarse_two = lax.psum_scatter(partial_two, "col", scatter_dimension=1, tiled=True).astype(
        jnp.bfloat16
    )
    group_two = lax.all_gather(coarse_two, "col", axis=1, tiled=True)
    segment_third = slot_layout(pointers_three, tiles_three.shape[0])[1]
    partial_three = group_products(
        tiles_three, group_two, columns_three, segment_third, pointers_three.shape[0] - 1
    )
    partial_three = add_points(partial_three, coarse_two, points_three, lax.axis_index("row"))
    coarse_three = lax.psum_scatter(partial_three, "row", scatter_dimension=1, tiled=True).astype(
        jnp.bfloat16
    )
    return (coarse_one, coarse_two, coarse_three)


def solution(mesh):
    placed = (
        P(None, ("row", "col")),
        P(("row", "col"), None, None),
        P(("row", "col")),
        P(("row", "col")),
        P(("col", "row")),
        P(("row", "col"), None, None),
        P(("row", "col")),
        P(("row", "col")),
        P(("row", "col")),
        P(("row", "col"), None, None),
        P(("row", "col")),
        P(("row", "col")),
        P(("col", "row")),
    )
    return jax.shard_map(
        on_device,
        mesh=mesh,
        in_specs=placed,
        out_specs=(P(None, ("col", "row")), P(None, ("row", "col")), P(None, ("col", "row"))),
        check_vma=False,
    )
```

profile of v0, /device:TPU:0, one launch (start us, length us, event | category | flops | bytes accessed | tf_op | source)
XLA Modules:
  0.0 434.2 jit_solution(3455119433022537755)
XLA Ops:
  7.2 1.3 slice.33
  8.5 0.7 add_compare_fusion
  9.2 0.7 iota_compare_fusion.5
  9.8 0.7 and_select_fusion
  10.5 0.6 reduce-window.6
  11.4 0.7 compare_select_fusion.5
  12.1 1.4 scatter_custom_fusion
  13.5 0.7 all_to_all.13
  14.2 5.2 %all-to-all-start = ((s32[8,1,32]{2,1,0:T(1,128)}), s32[8,1,32]{2,1,0:T(1,128)S(1)}, u32[]{:S(2)}, u32[]{:S(2)}) async-start(s32[8,1,32]{2,1,0:T(1,128)} %all_to_all.13), calls=%async_computation | async-start | bytes 8192 | tf_op jit(solution)/shard_map/all_to_all | solution.py:75
  19.4 1.1 bitcast_bitcast_fusion
  20.5 3.5 all-to-all-done
  24.1 0.8 gather_fusion
  25.0 1.3 broadcast_select_fusion
  26.2 3.6 all-to-all-start.1
  29.9 3.1 copy.76
  33.0 16.9 %gather_fusion.2 = bf16[4096,16]{1,0:T(8,128)(2,1)} fusion(bf16[16,16384]{0,1:T(8,128)(2,1)} %copy.76, s32[4096]{0:T(1024)S(1)} %fusion.16), kind=kCustom, calls=%fused_computation.2 | custom fusion | bytes 278528 | tf_op jit(solution)/shard_map/jit(_take)/gather | solution.py:34
  50.0 0.7 compare_and_fusion.6
  50.8 0.7 compare_select_fusion.7
  51.4 0.8 gather_fusion.1
  52.3 9.3 %fusion.1 = f32[256,16,128]{2,1,0:T(8,128)} fusion(bf16[256,128,128]{2,1,0:T(8,128)(2,1)} %param.14, bf16[256,16,128]{2,1,0:T(8,128)(2,1)S(1)} %gather_fusion.1, pred[256]{0:T(512)(128)(4,1)S(1)} %get-tuple-element.21), kind=kOutput, calls=%fused_computation.14 | convolution fusion | flops 134742016 | bytes 11534592 | tf_op jit(solution)/shard_map/sij,svj->svi/dot_general | solution.py:80
  61.6 20.6 %scatter_fusion = f32[129,16,128]{2,1,0:T(8,128)S(1)} fusion(f32[129,16,128]{2,1,0:T(8,128)S(1)} %broadcast_in_dim.121, s32[256]{0:T(256)S(1)} %bitcast.75, f32[256,16,128]{2,1,0:T(8,128)} %fusion.1), kind=kCustom, calls=%fused_computation.8 | custom fusion | flops 524288 | bytes 6292480 | tf_op jit(solution)/shard_map/scatter-add | solution.py:17
  82.3 4.6 %copy.94 = f32[16,128,128]{0,2,1:T(8,128)} copy(f32[16,128,128]{2,0,1:T(8,128)S(1)} %slice_bitcast_fusion) | data formatting | bytes 2097152 | tf_op jit(solution)/shard_map/reshape | solution.py:21
  87.0 3.0 fusion
  90.7 0.6 slice.38
  91.4 0.7 fusion.22
  92.1 144.5 %reduce-scatter.4.cloned.1.call-done = f32[16,4096]{0,1:T(8,128)} async-done(((f32[16,16384]{0,1:T(8,128)}), f32[16,4096]{0,1:T(8,128)}) %reduce-scatter.4.cloned.1.call-update) | async-done | bytes 262160 | tf_op jit(solution)/shard_map/reduce_scatter | solution.py:83
  236.6 1.7 convert_element_type.35
  238.3 72.1 %all_gather.6 = bf16[16,16384]{0,1:T(8,128)(2,1)} all-gather(bf16[16,4096]{0,1:T(8,128)(2,1)S(1)} %convert_element_type.35), channel_id=1, replica_groups=mesh['row'=4,'col'=8] {'row'}, dimensions={1}, use_global_device_ids=true | all-gather | bytes 655360 | tf_op jit(solution)/shard_map/all_gather | solution.py:86
  310.4 3.5 copy.79
  313.9 0.7 gather_fusion.3
  314.6 4.5 %fusion.5 = f32[128,16,128]{2,1,0:T(8,128)S(1)} fusion(bf16[128,128,128]{2,1,0:T(8,128)(2,1)} %param.18, bf16[128,16,128]{2,1,0:T(8,128)(2,1)S(1)} %gather_fusion.3, pred[128]{0:T(512)(128)(4,1)S(1)} %compare_and_fusion.5), kind=kOutput, calls=%fused_computation.22 | convolution fusion | flops 67371008 | bytes 5767296 | tf_op jit(solution)/shard_map/sij,vsj->svi/dot_general | solution.py:29
  319.2 5.5 %scatter_fusion.1 = f32[65,16,128]{2,1,0:T(8,128)S(1)} fusion(f32[65,16,128]{2,1,0:T(8,128)S(1)} %broadcast_in_dim.133, s32[128]{0:T(128)S(1)} %fusion.22, f32[128,16,128]{2,1,0:T(8,128)S(1)} %fusion.5), kind=kCustom, calls=%fused_computation.9 | custom fusion | flops 262144 | bytes 3146240 | tf_op jit(solution)/shard_map/scatter-add | solution.py:17
  324.8 2.6 copy.96
  327.3 3.2 gather_fusion.4
  330.6 2.0 fusion.4
  332.8 0.6 slice.41
  333.4 0.6 fusion.23
  334.1 50.5 %reduce-scatter.6.cloned.1.call-done = f32[16,1024]{0,1:T(8,128)} async-done(((f32[16,8192]{0,1:T(8,128)}), f32[16,1024]{0,1:T(8,128)}) %reduce-scatter.6.cloned.1.call-update) | async-done | bytes 65552 | tf_op jit(solution)/shard_map/reduce_scatter | solution.py:92
  384.6 1.1 convert_element_type.38
  385.7 15.3 %all_gather.7 = bf16[16,8192]{0,1:T(8,128)(2,1)} all-gather(bf16[16,1024]{0,1:T(8,128)(2,1)S(1)} %convert_element_type.38), channel_id=1, replica_groups=mesh['row'=4,'col'=8] {'col'}, dimensions={1}, use_global_device_ids=true | all-gather | bytes 294912 | tf_op jit(solution)/shard_map/all_gather | solution.py:95
  401.0 1.9 copy.84
  403.9 1.2 scatter_fusion.2
  405.2 0.9 gather_fusion.6
  406.2 0.6 copy-done.3
  406.9 1.0 copy.88
  407.8 0.7 copy.89
  408.6 17.8 %reduce-scatter.8.cloned.1.call-done = f32[16,256]{1,0:T(8,128)} async-done(((f32[16,1024]{1,0:T(8,128)}), f32[16,256]{1,0:T(8,128)}) %reduce-scatter.8.cloned.1.call-update) | async-done | bytes 16400 | tf_op jit(solution)/shard_map/reduce_scatter | solution.py:101
  426.4 1.3 convert_element_type.41
  (72 shorter events, 3.4 us)
Async XLA Ops:
  7.2 396.3 %copy-start = (bf16[16,128,128]{2,1,0:T(8,128)(2,1)S(1)}, bf16[16,128,128]{2,1,0:T(8,128)(2,1)}, u32[]{:S(2)}) copy-start(bf16[16,128,128]{2,1,0:T(8,128)(2,1)} %param.22) | copy-start | bytes 1572868
  7.2 22.7 %copy-start.7 = (s32[129]{0:T(256)S(1)}, s32[129]{0:T(256)}, u32[]{:S(2)}) copy-start(s32[129]{0:T(256)} %param.15) | copy-start | bytes 1552
  7.2 22.8 %copy-start.1 = (bf16[16,16384]{1,0:T(8,128)(2,1)S(1)}, bf16[16,16384]{1,0:T(8,128)(2,1)}, u32[]{:S(2)}) copy-start(bf16[16,16384]{1,0:T(8,128)(2,1)} %param.13) | copy-start | bytes 1572868
  7.2 22.6 %copy-start.4 = (s32[4096]{0:T(1024)S(1)}, s32[4096]{0:T(1024)}, u32[]{:S(2)}) copy-start(s32[4096]{0:T(1024)} %param.17) | copy-start | bytes 49156
  14.2 9.8 %all-to-all-start = ((s32[8,1,32]{2,1,0:T(1,128)}), s32[8,1,32]{2,1,0:T(1,128)S(1)}, u32[]{:S(2)}, u32[]{:S(2)}) async-start(s32[8,1,32]{2,1,0:T(1,128)} %all_to_all.13), calls=%async_computation | async-start | bytes 8192 | tf_op jit(solution)/shard_map/all_to_all | solution.py:75
  26.2 25.2 %all-to-all-start.1 = ((bf16[8,32,16,128]{3,2,1,0:T(8,128)(2,1)}), bf16[8,32,16,128]{3,2,1,0:T(8,128)(2,1)S(1)}, u32[]{:S(2)}, u32[]{:S(2)}) async-start(bf16[8,32,16,128]{3,2,1,0:T(8,128)(2,1)} %broadcast_select_fusion), calls=%async_computation.1 | async-start | bytes 2097152 | tf_op jit(solution)/shard_map/all_to_all | solution.py:77
  29.8 206.8 %reduce-scatter.4.cloned.1.call-start = ((), (), s32[]{:S(2)}) async-start(), calls=%async_computation.5 | async-start | bytes 10485760 | tf_op jit(solution)/shard_map/reduce_scatter | solution.py:83
  82.3 4.6 %copy-start.2 = (bf16[4096,16]{1,0:T(8,128)(2,1)S(1)}, bf16[4096,16]{1,0:T(8,128)(2,1)}, u32[]{:S(2)}) copy-start(bf16[4096,16]{1,0:T(8,128)(2,1)} %gather_fusion.2) | copy-start | bytes 393220
  89.9 0.7 copy-start.8
  89.9 1.3 copy-start.9
  89.9 1.3 copy-start.11
  89.9 2.1 copy-start.6
  89.9 2.1 copy-start.5
  90.0 294.7 %reduce-scatter.6.cloned.1.call-start = ((), (), s32[]{:S(2)}) async-start(), calls=%async_computation.6 | async-start | bytes 4718592 | tf_op jit(solution)/shard_map/reduce_scatter | solution.py:92
  324.7 7.9 %copy-start.10 = (s32[9]{0:T(128)S(1)}, s32[9]{0:T(128)}, u32[]{:S(2)}) copy-start(s32[9]{0:T(128)} %param.23) | copy-start | bytes 112
  332.6 93.8 %reduce-scatter.8.cloned.1.call-start = ((), (), s32[]{:S(2)}) async-start(), calls=%async_computation.7 | async-start | bytes 81920 | tf_op jit(solution)/shard_map/reduce_scatter | solution.py:101
  406.2 0.6 copy-start.3
Sparse Core Ops, SparseCore 0:
  90.1 146.4 reduce-scatter.3
  332.7 51.8 reduce-scatter.5
  407.0 19.3 reduce-scatter.7
where the time goes:
time: 435 us; the launch traced here: 434 us
  waiting for transfers between devices  216 us (50%)
  blocking collectives  87.4 us (20%)
  local copies, waits for them, and re-layouts  49.2 us (11%)
  other arithmetic  44.1 us (10%)
  matrix products  14.2 us (3%)
  between operations  14.2 us (3%)
  starting transfers between devices  8.88 us (2%)
    reduce_scatter x1, waiting for transfers between devices, on_device(): lax.psum_scatter(partial_one, 'row', scatter_dimension=1, tiled=True)  144 us
    all_gather x1, blocking collectives, on_device(): group_one = lax.all_gather(coarse_one, 'row', axis=1, tiled=True)  72.1 us
    reduce_scatter x1, waiting for transfers between devices, on_device(): lax.psum_scatter(partial_two, 'col', scatter_dimension=1, tiled=True)  50.5 us
    scatter-add x3, other arithmetic, block_sums(): jax.ops.segment_sum(products, segment, num_segments=block_count + 1, indi...  27.3 us
    gather x3, local copies, waits for them, and re-layouts, add_points(): injected = jnp.take(own_piece, points, axis=1).astype(jnp.float32)  21 us
    reduce_scatter x1, waiting for transfers between devices, on_device(): lax.psum_scatter(partial_three, 'row', scatter_dimension=1, tiled=True)  17.8 us
    all_gather x1, blocking collectives, on_device(): group_two = lax.all_gather(coarse_two, 'col', axis=1, tiled=True)  15.3 us
    dot_general x1, matrix products, on_device(): jnp.einsum('sij,svj->svi', tiles_one, picked, preferred_element_type=jnp....  9.25 us
  transfers between devices with their start and end apart: 5, of which 4 were waited for; matrix products, arithmetic and copies ran while one was open for 6% of the time, Pallas kernels for 0%

commit v1 on v0

--- a/solution.py
+++ b/solution.py
@@ -83,7 +83,12 @@
     coarse_one = lax.psum_scatter(partial_one, "row", scatter_dimension=1, tiled=True).astype(
         jnp.bfloat16
     )
-    group_one = lax.all_gather(coarse_one, "row", axis=1, tiled=True)
+    group_one = jnp.concatenate(
+        lax.all_to_all(
+            jnp.stack(tuple((coarse_one for _ in range(lax.axis_size("row"))))), "row", 0, 0
+        ),
+        1,
+    )
     segment_second = slot_layout(pointers_two, tiles_two.shape[0])[1]
     partial_two = group_products(
         tiles_two, group_one, columns_two, segment_second, pointers_two.shape[0] - 1

time: 435 us -> 374 us (0.86)
  blocking collectives: 87.4 us -> 14.1 us
  waiting for transfers between devices: 216 us -> 227 us
    all_gather x1 -> x0, blocking collectives: 72.1 us -> none  [on_device(): group_one = lax.all_gather(coarse_one, 'row', axis=1, tiled=True)]
    all_to_all x0 -> x1, waiting for transfers between devices: none -> 11.1 us  [on_device(): lax.all_to_all(jnp.stack(tuple((coarse_one for _ in range(lax.axis_size('...]
    reshape x2 -> x1, local copies, waits for them, and re-layouts: 5.37 us -> 0.79 us  [group_products(): fine_group.reshape(vector_count, fine_group.shape[1] // tile_edge, tile_e...]
  transfers between devices with their start and end apart: 5 -> 6, of which waited for: 4 -> 5; matrix products, arithmetic and copies ran while one was open for 6% -> 8% of each run, Pallas kernels for 0% -> 0%
where the time goes in v1:
time: 374 us; the launch traced here: 373 us
  waiting for transfers between devices  227 us (61%)
  local copies, waits for them, and re-layouts  46.1 us (12%)
  other arithmetic  44.1 us (12%)
  matrix products  14.2 us (4%)
  between operations  14.2 us (4%)
  blocking collectives  14.1 us (4%)
  starting transfers between devices  13.1 us (4%)
    reduce_scatter x1, waiting for transfers between devices, on_device(): lax.psum_scatter(partial_one, 'row', scatter_dimension=1, tiled=True)  145 us
    reduce_scatter x1, waiting for transfers between devices, on_device(): lax.psum_scatter(partial_two, 'col', scatter_dimension=1, tiled=True)  48.9 us
    scatter-add x3, other arithmetic, block_sums(): jax.ops.segment_sum(products, segment, num_segments=block_count + 1, indi...  27.3 us
    gather x3, local copies, waits for them, and re-layouts, add_points(): injected = jnp.take(own_piece, points, axis=1).astype(jnp.float32)  21 us
    reduce_scatter x1, waiting for transfers between devices, on_device(): lax.psum_scatter(partial_three, 'row', scatter_dimension=1, tiled=True)  18.9 us
    all_gather x1, blocking collectives, on_device(): group_two = lax.all_gather(coarse_two, 'col', axis=1, tiled=True)  14.1 us
    all_to_all x1, waiting for transfers between devices, on_device(): lax.all_to_all(jnp.stack(tuple((coarse_one for _ in range(lax.axis_size('...  11.1 us
    dot_general x1, matrix products, on_device(): jnp.einsum('sij,svj->svi', tiles_one, picked, preferred_element_type=jnp....  9.25 us
  transfers between devices with their start and end apart: 6, of which 5 were waited for; matrix products, arithmetic and copies ran while one was open for 8% of the time, Pallas kernels for 0%

profile of v1, /device:TPU:0, one launch (start us, length us, event | category | flops | bytes accessed | tf_op | source)
XLA Modules:
  0.0 372.8 jit_solution(10182373773209408730)
XLA Ops:
  7.2 1.3 slice.33
  8.5 0.7 add_compare_fusion
  9.2 0.7 iota_compare_fusion.5
  9.8 0.7 and_select_fusion
  10.5 0.6 reduce-window.6
  11.4 0.7 compare_select_fusion.5
  12.1 1.4 scatter_custom_fusion
  13.5 0.7 all_to_all.16
  14.2 5.2 %all-to-all-start = ((s32[8,1,32]{2,1,0:T(1,128)}), s32[8,1,32]{2,1,0:T(1,128)S(1)}, u32[]{:S(2)}, u32[]{:S(2)}) async-start(s32[8,1,32]{2,1,0:T(1,128)} %all_to_all.16), calls=%async_computation | async-start | bytes 8192 | tf_op jit(solution)/shard_map/all_to_all | solution.py:75
  19.4 1.1 bitcast_bitcast_fusion
  20.5 3.5 all-to-all-done
  24.1 0.8 gather_fusion
  25.0 1.3 broadcast_select_fusion
  26.2 3.6 all-to-all-start.1
  29.9 3.1 copy.81
  33.0 16.9 %gather_fusion.2 = bf16[4096,16]{1,0:T(8,128)(2,1)} fusion(bf16[16,16384]{0,1:T(8,128)(2,1)} %copy.81, s32[4096]{0:T(1024)S(1)} %fusion.16), kind=kCustom, calls=%fused_computation.2 | custom fusion | bytes 278528 | tf_op jit(solution)/shard_map/jit(_take)/gather | solution.py:34
  50.0 0.7 compare_and_fusion.6
  50.8 0.7 compare_select_fusion.7
  51.4 0.8 gather_fusion.1
  52.3 9.3 %fusion.1 = f32[256,16,128]{2,1,0:T(8,128)} fusion(bf16[256,128,128]{2,1,0:T(8,128)(2,1)} %param.14, bf16[256,16,128]{2,1,0:T(8,128)(2,1)S(1)} %gather_fusion.1, pred[256]{0:T(512)(128)(4,1)S(1)} %get-tuple-element.21), kind=kOutput, calls=%fused_computation.14 | convolution fusion | flops 134742016 | bytes 11534592 | tf_op jit(solution)/shard_map/sij,svj->svi/dot_general | solution.py:80
  61.6 20.6 %scatter_fusion = f32[129,16,128]{2,1,0:T(8,128)S(1)} fusion(f32[129,16,128]{2,1,0:T(8,128)S(1)} %broadcast_in_dim.121, s32[256]{0:T(256)S(1)} %bitcast.75, f32[256,16,128]{2,1,0:T(8,128)} %fusion.1), kind=kCustom, calls=%fused_computation.8 | custom fusion | flops 524288 | bytes 6292480 | tf_op jit(solution)/shard_map/scatter-add | solution.py:17
  82.3 4.6 %copy.98 = f32[16,128,128]{0,2,1:T(8,128)} copy(f32[16,128,128]{2,0,1:T(8,128)S(1)} %slice_bitcast_fusion) | data formatting | bytes 2097152 | tf_op jit(solution)/shard_map/reshape | solution.py:21
  87.0 3.0 fusion
  90.0 0.6 copy-done.9
  91.4 0.7 fusion.22
  92.0 144.5 %reduce-scatter.4.cloned.1.call-done = f32[16,4096]{0,1:T(8,128)} async-done(((f32[16,16384]{0,1:T(8,128)}), f32[16,4096]{0,1:T(8,128)}) %reduce-scatter.4.cloned.1.call-update) | async-done | bytes 262160 | tf_op jit(solution)/shard_map/reduce_scatter | solution.py:83
  236.6 1.7 convert_element_type.35
  238.6 0.8 stack.2
  239.4 4.3 %all-to-all-start.2 = ((bf16[4,16,4096]{2,1,0:T(8,128)(2,1)}), bf16[4,16,4096]{2,1,0:T(8,128)(2,1)S(1)}, u32[]{:S(2)}, u32[]{:S(2)}) async-start(bf16[4,16,4096]{2,1,0:T(8,128)(2,1)} %stack.2), calls=%async_computation.3 | async-start | bytes 1048576 | tf_op jit(solution)/shard_map/all_to_all | solution.py:87
  243.8 3.2 gather_fusion.4
  247.0 11.1 %all-to-all-done.2 = bf16[4,16,4096]{2,1,0:T(8,128)(2,1)S(1)} async-done(((bf16[4,16,4096]{2,1,0:T(8,128)(2,1)}), bf16[4,16,4096]{2,1,0:T(8,128)(2,1)S(1)}, u32[]{:S(2)}, u32[]{:S(2)}) %all-to-all-start.2) | async-done | bytes 524320 | tf_op jit(solution)/shard_map/all_to_all | solution.py:87
  259.5 0.7 gather_fusion.3
  260.2 4.5 %fusion.5 = f32[128,16,128]{2,1,0:T(8,128)S(1)} fusion(bf16[128,128,128]{2,1,0:T(8,128)(2,1)} %param.18, bf16[128,16,128]{2,1,0:T(8,128)(2,1)S(1)} %gather_fusion.3, pred[128]{0:T(512)(128)(4,1)S(1)} %compare_and_fusion.5), kind=kOutput, calls=%fused_computation.22 | convolution fusion | flops 67371008 | bytes 5767296 | tf_op jit(solution)/shard_map/sij,vsj->svi/dot_general | solution.py:29
  264.7 5.5 %scatter_fusion.1 = f32[65,16,128]{2,1,0:T(8,128)S(1)} fusion(f32[65,16,128]{2,1,0:T(8,128)S(1)} %broadcast_in_dim.133, s32[128]{0:T(128)S(1)} %fusion.22, f32[128,16,128]{2,1,0:T(8,128)S(1)} %fusion.5), kind=kCustom, calls=%fused_computation.9 | custom fusion | flops 262144 | bytes 3146240 | tf_op jit(solution)/shard_map/scatter-add | solution.py:17
  270.3 2.6 copy.100
  272.9 2.0 fusion.4
  275.1 0.6 slice.41
  275.8 0.6 fusion.23
  276.5 48.9 %reduce-scatter.6.cloned.1.call-done = f32[16,1024]{0,1:T(8,128)} async-done(((f32[16,8192]{0,1:T(8,128)}), f32[16,1024]{0,1:T(8,128)}) %reduce-scatter.6.cloned.1.call-update) | async-done | bytes 65552 | tf_op jit(solution)/shard_map/reduce_scatter | solution.py:97
  325.3 1.1 convert_element_type.38
  326.4 14.1 %all_gather.3 = bf16[16,8192]{0,1:T(8,128)(2,1)S(1)} all-gather(bf16[16,1024]{0,1:T(8,128)(2,1)S(1)} %convert_element_type.38), channel_id=1, replica_groups=mesh['row'=4,'col'=8] {'col'}, dimensions={1}, use_global_device_ids=true | all-gather | bytes 294912 | tf_op jit(solution)/shard_map/all_gather | solution.py:100
  340.5 0.8 copy.90
  342.4 1.2 scatter_fusion.2
  343.6 0.9 gather_fusion.6
  344.7 0.6 copy-done.4
  345.3 0.7 copy.95
  346.1 18.9 %reduce-scatter.8.cloned.1.call-done = f32[16,256]{1,0:T(8,128)} async-done(((f32[16,1024]{1,0:T(8,128)}), f32[16,256]{1,0:T(8,128)}) %reduce-scatter.8.cloned.1.call-update) | async-done | bytes 16400 | tf_op jit(solution)/shard_map/reduce_scatter | solution.py:106
  365.0 1.3 convert_element_type.41
  (78 shorter events, 4.9 us)
Async XLA Ops:
  7.2 334.7 %copy-start = (bf16[16,128,128]{2,1,0:T(8,128)(2,1)S(1)}, bf16[16,128,128]{2,1,0:T(8,128)(2,1)}, u32[]{:S(2)}) copy-start(bf16[16,128,128]{2,1,0:T(8,128)(2,1)} %param.22) | copy-start | bytes 1572868
  7.2 22.7 %copy-start.8 = (s32[129]{0:T(256)S(1)}, s32[129]{0:T(256)}, u32[]{:S(2)}) copy-start(s32[129]{0:T(256)} %param.15) | copy-start | bytes 1552
  7.2 22.8 %copy-start.1 = (bf16[16,16384]{1,0:T(8,128)(2,1)S(1)}, bf16[16,16384]{1,0:T(8,128)(2,1)}, u32[]{:S(2)}) copy-start(bf16[16,16384]{1,0:T(8,128)(2,1)} %param.13) | copy-start | bytes 1572868
  7.2 22.6 %copy-start.5 = (s32[4096]{0:T(1024)S(1)}, s32[4096]{0:T(1024)}, u32[]{:S(2)}) copy-start(s32[4096]{0:T(1024)} %param.17) | copy-start | bytes 49156
  14.2 9.8 %all-to-all-start = ((s32[8,1,32]{2,1,0:T(1,128)}), s32[8,1,32]{2,1,0:T(1,128)S(1)}, u32[]{:S(2)}, u32[]{:S(2)}) async-start(s32[8,1,32]{2,1,0:T(1,128)} %all_to_all.16), calls=%async_computation | async-start | bytes 8192 | tf_op jit(solution)/shard_map/all_to_all | solution.py:75
  26.2 25.2 %all-to-all-start.1 = ((bf16[8,32,16,128]{3,2,1,0:T(8,128)(2,1)}), bf16[8,32,16,128]{3,2,1,0:T(8,128)(2,1)S(1)}, u32[]{:S(2)}, u32[]{:S(2)}) async-start(bf16[8,32,16,128]{3,2,1,0:T(8,128)(2,1)} %broadcast_select_fusion), calls=%async_computation.1 | async-start | bytes 2097152 | tf_op jit(solution)/shard_map/all_to_all | solution.py:77
  29.8 206.8 %reduce-scatter.4.cloned.1.call-start = ((), (), s32[]{:S(2)}) async-start(), calls=%async_computation.6 | async-start | bytes 10485760 | tf_op jit(solution)/shard_map/reduce_scatter | solution.py:83
  82.3 4.6 %copy-start.2 = (bf16[4096,16]{1,0:T(8,128)(2,1)S(1)}, bf16[4096,16]{1,0:T(8,128)(2,1)}, u32[]{:S(2)}) copy-start(bf16[4096,16]{1,0:T(8,128)(2,1)} %gather_fusion.2) | copy-start | bytes 393220
  89.9 0.7 copy-start.9
  89.9 1.4 copy-start.10
  89.9 1.4 copy-start.12
  90.6 153.2 %copy-start.7 = (s32[256]{0:T(256)S(1)}, s32[256]{0:T(256)}, u32[]{:S(2)}) copy-start(s32[256]{0:T(256)} %param.25) | copy-start | bytes 3076
  90.6 153.2 %copy-start.6 = (s32[1024]{0:T(1024)S(1)}, s32[1024]{0:T(1024)}, u32[]{:S(2)}) copy-start(s32[1024]{0:T(1024)} %param.21) | copy-start | bytes 12292
  238.6 26.1 %copy-start.3 = (bf16[16,4096]{1,0:T(8,128)(2,1)}, bf16[16,4096]{1,0:T(8,128)(2,1)S(1)}, u32[]{:S(2)}) copy-start(bf16[16,4096]{1,0:T(8,128)(2,1)S(1)} %copy.94) | copy-start | bytes 393220
  239.4 18.7 %all-to-all-start.2 = ((bf16[4,16,4096]{2,1,0:T(8,128)(2,1)}), bf16[4,16,4096]{2,1,0:T(8,128)(2,1)S(1)}, u32[]{:S(2)}, u32[]{:S(2)}) async-start(bf16[4,16,4096]{2,1,0:T(8,128)(2,1)} %stack.2), calls=%async_computation.3 | async-start | bytes 1048576 | tf_op jit(solution)/shard_map/all_to_all | solution.py:87
  243.7 81.6 %reduce-scatter.6.cloned.1.call-start = ((), (), s32[]{:S(2)}) async-start(), calls=%async_computation.7 | async-start | bytes 4718592 | tf_op jit(solution)/shard_map/reduce_scatter | solution.py:97
  270.3 4.7 %copy-start.11 = (s32[9]{0:T(128)S(1)}, s32[9]{0:T(128)}, u32[]{:S(2)}) copy-start(s32[9]{0:T(128)} %param.23) | copy-start | bytes 112
  275.0 90.0 %reduce-scatter.8.cloned.1.call-start = ((), (), s32[]{:S(2)}) async-start(), calls=%async_computation.8 | async-start | bytes 81920 | tf_op jit(solution)/shard_map/reduce_scatter | solution.py:106
  344.7 0.6 copy-start.4
Sparse Core Ops, SparseCore 0:
  90.1 146.4 reduce-scatter.3
  275.1 50.1 reduce-scatter.5
  345.5 19.4 reduce-scatter.7
